TPU v7x, 8 devices: a whole 2x2x1 slice. The times are simulated.
8 devices in a mesh: dp: 1 (over z), tp: 2 (over y), ep: 4 (over x, core).
Axes of the slice: x: 2, y: 2, z: 1, core: 2. Of those that a mesh axis runs over, the one named last changes fastest.
Arguments:
- tokens: bfloat16 [16384, 2048], P(('dp', 'ep'))
- expert_ids: int32 [16384, 2], P(('dp', 'ep'))
- norm_gain: bfloat16 [2048], replicated
- router_w: bfloat16 [2048, 8], replicated
- w_gate: bfloat16 [8, 2048, 5632], P('ep', None, 'tp')
- w_up: bfloat16 [8, 2048, 5632], P('ep', None, 'tp')
- w_down: bfloat16 [8, 5632, 2048], P('ep', 'tp')
Outputs:
- output: bfloat16 [16384, 2048], P(('dp', 'ep'))
All inputs are finite; a program needn't handle non-finite values.
Results may differ from a plain program's by a relative error of at most 0.012134.
Values are sent between devices in bfloat16 or wider.
A program may use at most 1 GiB of HBM per device.

v0:
```python
import functools

import jax
import jax.numpy as jnp
from jax import lax
from jax.experimental import pallas as pl
from jax.experimental.pallas import tpu as pltpu
from jax.sharding import PartitionSpec as P


NORM_EPS = 1e-5
ALIGN = 16
PIECE = 512
SUB = 128
TILE = 512
FCH = 256
RP = 2304
ANY = pl.BlockSpec(memory_space=pl.ANY)
SMEM = pl.BlockSpec(memory_space=pltpu.SMEM)
VMEM = pl.BlockSpec(memory_space=pltpu.VMEM)
PICK = 1152
TIERS = (688, 736, 784, 848, 1088)


def count_at(cnt, block, exp, quarter, half):
    return cnt[((block * 8 + exp) * 4 + quarter) * 2 + half]


def padded(c):
    return (c + (ALIGN - 1)) // ALIGN * ALIGN


def ffn_kernel(rel, q0, n, groups, pos_ref, cnt_ref, rank_ref, *refs):
    ng = len(groups)
    toks, ws = refs[:n], [refs[n + 3 * i:n + 3 * i + 3] for i in range(ng)]
    outs, (tokb, hbuf, acc, b1, b3, b2, tsem, wsem, osem) = refs[-9 - 2 * n:-9], refs[-9:]
    me, half = pos_ref[0], pos_ref[1]
    block = me ^ rel
    nf = ws[0][0].shape[2] // FCH
    ntok = 2 * PIECE

    def w_copies(w, g):
        e, f, s = g // nf % 2, g % nf, g % 2
        cols = pl.ds(pl.multiple_of(f * FCH, FCH), FCH)
        return (pltpu.make_async_copy(w[0].at[e, :, cols], b1.at[s], wsem.at[s, 0]),
                pltpu.make_async_copy(w[1].at[e, :, cols], b3.at[s], wsem.at[s, 1]),
                pltpu.make_async_copy(w[2].at[e, cols, :], b2.at[s], wsem.at[s, 2]))

    def w_start(g):
        for i, w in enumerate(ws):
            @pl.when(g // (2 * nf) == i)
            def _():
                for c in w_copies(w, g):
                    c.start()

    def tok_copy(a):
        return pltpu.make_async_copy(toks[a], tokb.at[pl.ds(a * ntok, ntok)], tsem.at[a])

    for a in range(n):
        tok_copy(a).start()
    w_start(jnp.int32(0))
    for a in range(n):
        tok_copy(a).wait()

    def expert(e, bases):
        g_dev = groups[0] + e // 2
        exp = 2 * (me ^ g_dev) + e % 2

        def piece(p, row):
            t, a = jnp.where(p < n, 1 - half, half), p % n
            c = count_at(cnt_ref, block, exp, q0 + a, t)
            ranks = rank_ref[pl.ds(((rel // 2 * 4 + g_dev * 2 + e % 2) * 4 + q0 + a) * 2 + t, 1), :]
            tok = pl.ds(pl.multiple_of(a * ntok + t * PIECE, PIECE), PIECE)

            def sub(s, _):
                rows = lax.broadcasted_iota(jnp.int32, (SUB, PIECE), 0) + s * SUB
                sel = jnp.where(rows == ranks, 1.0, 0.0).astype(jnp.bfloat16)
                got = jnp.dot(sel, tokb[tok, :], preferred_element_type=jnp.float32)
                hbuf[pl.ds(pl.multiple_of(row + s * SUB, ALIGN), SUB), :] = got.astype(jnp.bfloat16)
                return 0

            lax.fori_loop(0, (c + SUB - 1) // SUB, sub, 0)
            return row + padded(c)

        total = lax.fori_loop(0, 2 * n, piece, jnp.int32(0))
        half_tile = TILE // 2
        nt = (total + half_tile - 1) // TILE
        rest = total > nt * TILE

        def tile(j, rows=TILE):
            return pl.ds(pl.multiple_of(j * TILE, TILE), rows)

        def over_tiles(do):
            pl.loop(0, nt)(lambda j: do(tile(j)))
            pl.when(rest)(lambda: do(tile(nt, half_tile)))

        def clear(at):
            acc[at, :] = jnp.zeros((at.size, acc.shape[1]), jnp.float32)

        over_tiles(clear)

        def width(f, _):
            g = e * nf + f
            s = g % 2

            w_start(g + 1)
            for c in w_copies(ws[0], g):
                c.wait()

            def rows(at):
                h = hbuf[at, :]
                a = jnp.dot(h, b1[s], preferred_element_type=jnp.float32)
                b = jnp.dot(h, b3[s], preferred_element_type=jnp.float32)
                u = (jax.nn.silu(a) * b).astype(jnp.bfloat16)
                acc[at, :] += jnp.dot(u, b2[s], preferred_element_type=jnp.float32)

            over_tiles(rows)
            return 0

        lax.fori_loop(0, nf, width, 0)

        def cast(at):
            hbuf[at, :] = acc[at, :].astype(jnp.bfloat16)

        over_tiles(cast)
        ends, lo = [], jnp.int32(0)
        places = []
        for p in range(2 * n):
            size = padded(count_at(cnt_ref, block, exp, q0 + p % n, 1 - half if p < n else half))
            places.append((outs[p], bases[p], lo, size))
            ends.append(bases[p] + size)
            lo += size
        for wait in (False, True):
            for dst, base, lo, size in places:
                whole = size // SUB

                def copy(at, rows):
                    c = pltpu.make_async_copy(hbuf.at[pl.ds(pl.multiple_of(lo + at, ALIGN), rows)],
                                              dst.at[pl.ds(pl.multiple_of(base + at, ALIGN), rows)], osem)
                    c.wait() if wait else c.start()

                pl.loop(0, whole)(lambda j: copy(j * SUB, SUB))
                pl.loop(0, (size - whole * SUB) // ALIGN)(lambda j: copy(whole * SUB + j * ALIGN, ALIGN))
        return tuple(ends)

    start = []
    for p in range(2 * n):
        at = jnp.int32(0)
        if groups[0]:
            for e in range(2):
                at += padded(count_at(cnt_ref, block, 2 * me + e, q0 + p % n, 1 - half if p < n else half))
        start.append(at)
    lax.fori_loop(0, 2 * ng, expert, tuple(start))


def run_ffn(rel, q0, n, groups, cap, pos, cnt, ranks, toks, weights, into=()):
    dim, width = weights[0][0].shape[1:]
    rows = 512 * n * len(groups)
    flat = [w for ws in weights for w in ws]
    n_in = 3 + n + len(flat)
    kern = functools.partial(ffn_kernel, rel, q0, n, groups)
    if into:
        def kern(*refs):
            ffn_kernel(rel, q0, n, groups, *refs[:n_in], *refs[n_in + 2 * n:])
    return pl.pallas_call(
        kern,
        out_shape=[jax.ShapeDtypeStruct((cap, dim), jnp.bfloat16)] * (2 * n),
        in_specs=[SMEM, SMEM, VMEM] + [ANY] * (n + len(flat) + len(into)),
        out_specs=[ANY] * (2 * n),
        input_output_aliases={n_in + i: i for i in range(len(into))},
        scratch_shapes=[
            pltpu.VMEM((n * 2 * PIECE, dim), jnp.bfloat16),
            pltpu.VMEM((RP, dim), jnp.bfloat16),
            pltpu.VMEM((RP, dim), jnp.float32),
            pltpu.VMEM((2, dim, FCH), jnp.bfloat16),
            pltpu.VMEM((2, dim, FCH), jnp.bfloat16),
            pltpu.VMEM((2, FCH, dim), jnp.bfloat16),
            pltpu.SemaphoreType.DMA((n,)),
            pltpu.SemaphoreType.DMA((2, 3)),
            pltpu.SemaphoreType.DMA,
        ],
        compiler_params=pltpu.CompilerParams(vmem_limit_bytes=62 * 1024 * 1024),
        cost_estimate=pl.CostEstimate(flops=rows * 6 * dim * width, bytes_accessed=6 * dim * width * 2 * len(groups), transcendentals=0),
    )(pos, cnt, ranks, *toks, *flat, *into)


def mix_kernel(quarter, pos_ref, cnt_ref, ranks, ids, gates, tokens, own, far, out, rb, xb, sem, xsem):
    me, half = pos_ref[0], pos_ref[1]
    dim = out.shape[1]
    row0 = quarter * 2 * PIECE + half * PIECE
    x_copy = pltpu.make_async_copy(tokens.at[pl.ds(pl.multiple_of(row0, PIECE), PIECE)], xb, xsem)
    x_copy.start()

    moves, shifts = [], []
    to = jnp.int32(0)
    for r, buf in ((0, own), (2, far)):
        at = jnp.int32(0)
        for g in range(2):
            for e in range(2):
                exp = 2 * (me ^ (r + g)) + e
                size = padded(count_at(cnt_ref, me, exp, quarter, half))
                moves.append((buf, at, to, size))
                shifts.append((exp, to))
                at += size
                to += size

    for wait in (False, True):
        for buf, src, dst, size in moves:
            whole = size // SUB

            def copy(off, rows):
                c = pltpu.make_async_copy(buf.at[pl.ds(pl.multiple_of(src + off, ALIGN), rows)],
                                          rb.at[pl.ds(pl.multiple_of(dst + off, ALIGN), rows)], sem)
                c.wait() if wait else c.start()

            pl.loop(0, whole)(lambda j: copy(j * SUB, SUB))
            pl.loop(0, (size - whole * SUB) // ALIGN)(lambda j: copy(whole * SUB + j * ALIGN, ALIGN))
    x_copy.wait()

    tail = pl.ds(2 * PIECE, PICK - 2 * PIECE)
    valid = lax.broadcasted_iota(jnp.int32, (PICK - 2 * PIECE, dim), 0) + 2 * PIECE < to
    rb[tail, :] = jnp.where(valid, rb[tail, :].astype(jnp.float32), 0.0).astype(jnp.bfloat16)

    lane = lax.broadcasted_iota(jnp.int32, ranks.shape, 1)
    places = ranks[...]
    for exp, shift in shifts:
        places += jnp.where(lane == exp, shift, 0)
    n_col = 512
    sels = []
    for k in range(2):
        place = jnp.sum(jnp.where(lane == ids[:, k:k + 1], places, 0), axis=1, keepdims=True)
        col = lax.broadcasted_iota(jnp.int32, (PIECE, PICK), 1)
        sels.append(jnp.where(col == place, 1.0, 0.0).astype(jnp.bfloat16))
    for c in range(0, dim, n_col):
        cols = slice(c, c + n_col)
        mixed = xb[:, cols].astype(jnp.float32)
        for k in range(2):
            mixed += gates[:, k:k + 1] * jnp.dot(sels[k], rb[:, cols], preferred_element_type=jnp.float32)
        out[:, cols] = mixed.astype(out.dtype)


def run_mix(quarter, pos, cnt, ranks, ids, gates, tokens, own, far):
    dim = tokens.shape[1]
    return pl.pallas_call(
        functools.partial(mix_kernel, quarter),
        out_shape=jax.ShapeDtypeStruct((PIECE, dim), tokens.dtype),
        in_specs=[SMEM, SMEM, VMEM, VMEM, VMEM, ANY, ANY, ANY],
        out_specs=VMEM,
        scratch_shapes=[pltpu.VMEM((PICK, dim), jnp.bfloat16), pltpu.VMEM((PIECE, dim), jnp.bfloat16), pltpu.SemaphoreType.DMA, pltpu.SemaphoreType.DMA],
        cost_estimate=pl.CostEstimate(flops=4 * PIECE * PICK * dim, bytes_accessed=4 * PICK * dim, transcendentals=0),
    )(pos, cnt, ranks, ids, gates, tokens, own, far)


def tier_kernel(caps, cnt_ref, out):
    def group(i, m):
        block, chip, quarter, half = i // 16, i // 8 % 2, i // 2 % 4, i % 2
        return jnp.maximum(m, sum(padded(count_at(cnt_ref, block, 4 * chip + e, quarter, half)) for e in range(4)))

    need = lax.fori_loop(0, 64, group, jnp.int32(0))
    out[0] = sum(jnp.where(need > cap, 1, 0) for cap in caps[:-1])


def run_tier(cnt, caps):
    return pl.pallas_call(functools.partial(tier_kernel, caps), out_shape=jax.ShapeDtypeStruct((1,), jnp.int32), in_specs=[SMEM], out_specs=SMEM, name="tier")(cnt)


def solution(mesh):
    tok_spec = P(('dp', 'ep'), None)
    swap_x = [(0, 2), (2, 0), (1, 3), (3, 1)]
    swap_c = [(0, 1), (1, 0), (2, 3), (3, 2)]

    def local_block(tokens, expert_ids, norm_gain, router_w, w_gate, w_up, w_down):
        num_tok, _ = tokens.shape
        quarter = num_tok // 4
        gain = norm_gain.astype(jnp.float32)
        me = lax.axis_index('ep').astype(jnp.int32)
        half = lax.axis_index('tp').astype(jnp.int32)
        pos = jnp.stack([me, half])

        own_h, logits = [], []
        for q in range(4):
            x = tokens[q * quarter:(q + 1) * quarter].astype(jnp.float32)
            inv = lax.rsqrt(jnp.mean(x * x, axis=-1, keepdims=True) + NORM_EPS)
            h = (x * inv * gain).astype(jnp.bfloat16)
            own_h.append(h)
            logits.append(jnp.dot(h, router_w, preferred_element_type=jnp.float32))
        logits = jnp.concatenate(logits, axis=0)
        exps = jnp.arange(8, dtype=jnp.int32)
        hit = expert_ids[:, :, None] == exps[None, None, :]
        gates = jax.nn.softmax(jnp.sum(jnp.where(hit, logits[:, None, :], 0.0), axis=-1), axis=-1)

        ids = lax.all_gather(expert_ids.T, 'ep')
        chosen = (ids[:, 0, None, :] == exps[None, :, None]) | (ids[:, 1, None, :] == exps[None, :, None])
        cnt = jnp.sum(chosen.reshape(4, 8, 8, PIECE).astype(jnp.int32), axis=-1).reshape(-1)
        tri = (jnp.arange(PIECE)[:, None] < jnp.arange(PIECE)[None, :]).astype(jnp.bfloat16)

        def ranked(picked):
            before = jnp.dot(picked.astype(jnp.bfloat16), tri, preferred_element_type=jnp.float32)
            return jnp.where(picked, before.astype(jnp.int32), -1)

        ids_rel = ids[me ^ jnp.array([0, 2], jnp.int32)]
        mine = jnp.stack([2 * me, 2 * me + 1, 2 * (me ^ 1), 2 * (me ^ 1) + 1])
        picked = (ids_rel[:, 0, None, :] == mine[None, :, None]) | (ids_rel[:, 1, None, :] == mine[None, :, None])
        rank_in = ranked(picked.reshape(64, PIECE))
        own_picked = jnp.any(hit, axis=1).T
        rank_own = ranked(own_picked.reshape(64, PIECE)).reshape(8, num_tok).T

        def body(cap, tokens, own_h, pos, cnt, rank_in, rank_own, ids_own, gates, w_gate, w_up, w_down):
            far_h = [lax.ppermute(h, 'ep', swap_x) for h in own_h]
            mine = (w_gate, w_up, w_down)
            theirs = tuple(lax.ppermute(w, 'ep', swap_c) for w in mine)
            half = pos[1]
            out = jnp.zeros_like(tokens)
            pieces = []

            def ffn(rel, q0, n, groups, after, into=()):
                first = lax.optimization_barrier((pos, *after))[0]
                src = (own_h, far_h)[rel // 2][q0:q0 + n]
                return run_ffn(rel, q0, n, groups, cap, first, cnt, rank_in, src, [(mine, theirs)[g] for g in groups], into)

            def swap_tp(send):
                return lax.ppermute(send, 'tp', [(0, 1), (1, 0)])

            def reduce(send, keep):
                got = swap_tp(send)
                return (keep.astype(jnp.float32) + got.astype(jnp.float32)).astype(jnp.bfloat16)

            def mix(q, own, far):
                piece = run_mix(q, pos, cnt, rank_own[q], ids_own[q], gates[q], tokens, own, far)
                pieces.append((piece, lax.ppermute(piece, 'tp', [(0, 1), (1, 0)])))

            a = ffn(0, 0, 4, (0,), ())
            send, keep = a[:4], a[4:]
            a0 = ffn(0, 0, 2, (1,), a[:1], (*send[:2], *keep[:2]))
            own = [reduce(a0[i], a0[2 + i]) for i in range(2)]
            a1 = ffn(0, 2, 2, (1,), a0[:1], (*send[2:], *keep[2:]))
            own += [reduce(a1[i], a1[2 + i]) for i in range(2)]
            b0 = ffn(2, 0, 2, (0, 1), a1[:1])
            far = [reduce(b0[i], b0[2 + i]) for i in range(2)]
            b1 = ffn(2, 2, 2, (0, 1), b0[:1])
            late = [swap_tp(b1[i]) for i in range(2)]
            back = [lax.ppermute(rows, 'ep', swap_x) for rows in far]
            for i in range(2):
                mix(i, own[i], back[i])
                keep, got, _ = lax.optimization_barrier((b1[2 + i], late[i], pieces[i][0]))
                back.append(lax.ppermute((keep.astype(jnp.float32) + got.astype(jnp.float32)).astype(jnp.bfloat16), 'ep', swap_x))
            for q in range(2, 4):
                mix(q, own[q], back[q])
            for q, (piece, other) in enumerate(pieces):
                out = lax.dynamic_update_slice(out, piece, (q * quarter + half * PIECE, 0))
                out = lax.dynamic_update_slice(out, other, (q * quarter + (1 - half) * PIECE, 0))
            return out

        def own_half(v):
            return lax.dynamic_index_in_dim(v.reshape(4, 2, PIECE, -1), half, 1, keepdims=False)

        args = (tokens, own_h, pos, cnt, rank_in, own_half(rank_own), own_half(expert_ids), own_half(gates), w_gate, w_up, w_down)
        tier = run_tier(cnt, TIERS)

        def branch(i, *a):
            return body(TIERS[i], *a)

        return lax.switch(tier[0], [functools.partial(branch, i) for i in range(len(TIERS))], *args)

    return jax.shard_map(local_block, mesh=mesh, in_specs=(tok_spec, tok_spec, P(None), P(None, None), P('ep', None, 'tp'), P('ep', None, 'tp'), P('ep', 'tp', None)), out_specs=tok_spec, check_vma=False)
```

profile of v0, /device:TPU:6, one launch (start us, length us, event | category | flops | bytes accessed | tf_op | source)
XLA Modules:
  0.0 1175.3 jit_solution(4801019601418007827)
XLA Ops:
  0.0 7.7 fusion.15
  10.6 5.5 fusion.17
  27.0 7.5 all-gather.1
  39.1 4.2 tier.1
  43.9 1130.3 %conditional.1 = (bf16[4096,2048]{1,0:T(8,128)(2,1)}) conditional(s32[]{:T(128)} %bitcast.77, (s32[4096,8]{1,0:T(8,128)}, s32[4096,2]{0,1:T(2,128)}, f32[4096,2]{0,1:T(2,128)S(1)}, s32[2]{0:T(128)S(1)}, s32[256]{0:T(256)S(1)}, /*index=5*/pred[64,512]{1,0:T(32,128)(4,1)S(1)}, bf16[1024,2048]{1,0:T(8,128)(2,1)}, ...), branch_computations={%region_9.10_spmd, %region_10.11_spmd, %region_11.12_spmd, %region... | conditional | flops 302866563072 | bytes 1342292480 | solution.py:363
  55.7 116.6 %branch_1_fun.9 = (bf16[736,2048]{1,0:T(8,128)(2,1)}, bf16[736,2048]{1,0:T(8,128)(2,1)}, bf16[736,2048]{1,0:T(8,128)(2,1)}, bf16[736,2048]{1,0:T(8,128)(2,1)}, b...) custom-call(s32[2]{0:T(128)S(1)} %get-tuple-element.244.pos_ref.refs, ...), custom_call_target="tpu_custom_call" | custom-call | flops 70866960384 | bytes 69206016 | tf_op jit(solution)/shard_map/cond/branch_1_fun/pallas_call | solution.py:165
  174.3 102.7 %branch_1_fun.10 = (bf16[736,2048]{1,0:T(8,128)(2,1)}, bf16[736,2048]{1,0:T(8,128)(2,1)}, bf16[736,2048]{1,0:T(8,128)(2,1)}, bf16[736,2048]{1,0:T(8,128)(2,1)}) custom-call(s32[2]{0:T(128)S(1)} %get-tuple-element.244.pos_ref.refs_0_, ...), custom_call_target="tpu_custom_call", output_to_operand_aliasing={{0}: (8, {}), {1}: (9, {}), {2}: (10, {}), {3}: (11, {})} | custom-call | flops 35433480192 | bytes 69206016 | tf_op jit(solution)/shard_map/cond/branch_1_fun/pallas_call | solution.py:165
  277.1 102.4 %branch_1_fun.11 = (bf16[736,2048]{1,0:T(8,128)(2,1)}, bf16[736,2048]{1,0:T(8,128)(2,1)}, bf16[736,2048]{1,0:T(8,128)(2,1)}, bf16[736,2048]{1,0:T(8,128)(2,1)}) custom-call(s32[2]{0:T(128)S(1)} %get-tuple-element.244.pos_ref.refs_0_, ...), custom_call_target="tpu_custom_call", output_to_operand_aliasing={{0}: (8, {}), {1}: (9, {}), {2}: (10, {}), {3}: (11, {})} | custom-call | flops 35433480192 | bytes 69206016 | tf_op jit(solution)/shard_map/cond/branch_1_fun/pallas_call | solution.py:165
  379.6 133.1 %branch_1_fun.12 = (bf16[736,2048]{1,0:T(8,128)(2,1)}, bf16[736,2048]{1,0:T(8,128)(2,1)}, bf16[736,2048]{1,0:T(8,128)(2,1)}, bf16[736,2048]{1,0:T(8,128)(2,1)}) custom-call(s32[2]{0:T(128)S(1)} %get-tuple-element.244.pos_ref.refs_0_, s32[256]{0:T(256)S(1)} %get-tuple-element.209.cnt_ref.refs_1_, s32[64,512]{1,0:T(8,128)} %select_n.148.rank_ref.refs_2_, ...), custom_call_target="tpu_custom_call" | custom-call | flops 70866960384 | bytes 138412032 | tf_op jit(solution)/shard_map/cond/branch_1_fun/pallas_call | solution.py:165
  518.3 62.9 %collective-permute-done.29 = bf16[736,2048]{1,0:T(8,128)(2,1)} collective-permute-done((bf16[736,2048]{1,0:T(8,128)(2,1)}, bf16[736,2048]{1,0:T(8,128)(2,1)}, u32[]{:S(2)}, u32[]{:S(2)}) %collective-permute-start.29) | collective-permute-done | bytes 3014688 | tf_op jit(solution)/shard_map/cond/branch_1_fun/ppermute | solution.py:322
  581.2 6.0 add_convert_fusion.14
  587.2 129.7 %branch_1_fun.15 = (bf16[736,2048]{1,0:T(8,128)(2,1)}, bf16[736,2048]{1,0:T(8,128)(2,1)}, bf16[736,2048]{1,0:T(8,128)(2,1)}, bf16[736,2048]{1,0:T(8,128)(2,1)}) custom-call(s32[2]{0:T(128)S(1)} %get-tuple-element.244.pos_ref.refs_0_, s32[256]{0:T(256)S(1)} %get-tuple-element.209.cnt_ref.refs_1_, s32[64,512]{1,0:T(8,128)} %select_n.148.rank_ref.refs_2_, ...), custom_call_target="tpu_custom_call" | custom-call | flops 70866960384 | bytes 138412032 | tf_op jit(solution)/shard_map/cond/branch_1_fun/pallas_call | solution.py:165
  718.9 6.0 add_convert_fusion.12
  728.4 4.9 add_convert_fusion.13.own
  734.9 4.7 add_convert_fusion.15.own
  740.1 11.9 %branch_1_fun.13 = bf16[512,2048]{1,0:T(8,128)(2,1)} custom-call(s32[2]{0:T(128)S(1)} %get-tuple-element.244.pos_ref.refs_0_, s32[256]{0:T(256)S(1)} %get-tuple-element.209.cnt_ref.refs_1_, s32[512,8]{1,0:T(8,128)} %get-tuple-element.1024.ranks, s32[512,2]{1,0:T(8,128)} %get-tuple-element.1020.ids, f32[512,2]{1,0:T(8,128)} %get-tuple-element.1027.gates, ...), custom_call_target="tpu_custom_call" | custom-call | flops 4831838208 | bytes 9437184 | tf_op jit(solution)/shard_map/cond/branch_1_fun/pallas_call | solution.py:244
  752.0 39.5 %collective-permute-done.39 = bf16[736,2048]{1,0:T(8,128)(2,1)} collective-permute-done((bf16[736,2048]{1,0:T(8,128)(2,1)}, bf16[736,2048]{1,0:T(8,128)(2,1)}, u32[]{:S(2)}, u32[]{:S(2)}) %collective-permute-start.39) | collective-permute-done | bytes 3014688 | tf_op jit(solution)/shard_map/cond/branch_1_fun/ppermute | solution.py:322
  791.5 4.7 add_convert_fusion.10
  796.2 11.8 %branch_1_fun.14 = bf16[512,2048]{1,0:T(8,128)(2,1)} custom-call(s32[2]{0:T(128)S(1)} %get-tuple-element.244.pos_ref.refs_0_, s32[256]{0:T(256)S(1)} %get-tuple-element.209.cnt_ref.refs_1_, s32[512,8]{1,0:T(8,128)} %get-tuple-element.1023.ranks, s32[512,2]{1,0:T(8,128)} %get-tuple-element.1019.ids, f32[512,2]{1,0:T(8,128)} %get-tuple-element.1026.gates, ...), custom_call_target="tpu_custom_call" | custom-call | flops 4831838208 | bytes 9437184 | tf_op jit(solution)/shard_map/cond/branch_1_fun/pallas_call | solution.py:244
  808.1 48.0 %collective-permute-done.43 = bf16[736,2048]{1,0:T(8,128)(2,1)} collective-permute-done((bf16[736,2048]{1,0:T(8,128)(2,1)}, bf16[736,2048]{1,0:T(8,128)(2,1)}, u32[]{:S(2)}, u32[]{:S(2)}) %collective-permute-start.43) | collective-permute-done | bytes 3014688 | tf_op jit(solution)/shard_map/cond/branch_1_fun/ppermute | solution.py:322
  856.1 6.1 add_convert_fusion.8
  862.2 58.5 %collective-permute-done.36 = bf16[736,2048]{1,0:T(8,128)(2,1)} collective-permute-done((bf16[736,2048]{1,0:T(8,128)(2,1)}, bf16[736,2048]{1,0:T(8,128)(2,1)}, u32[]{:S(2)}, u32[]{:S(2)}) %collective-permute-start.36) | collective-permute-done | bytes 3014688 | tf_op jit(solution)/shard_map/cond/branch_1_fun/ppermute | solution.py:322
  920.7 4.7 add_convert_fusion.11.own
  925.5 11.9 %branch_1_fun.16 = bf16[512,2048]{1,0:T(8,128)(2,1)} custom-call(s32[2]{0:T(128)S(1)} %get-tuple-element.244.pos_ref.refs_0_, s32[256]{0:T(256)S(1)} %get-tuple-element.209.cnt_ref.refs_1_, s32[512,8]{1,0:T(8,128)} %get-tuple-element.1022.ranks, s32[512,2]{1,0:T(8,128)} %get-tuple-element.1018.ids, f32[512,2]{1,0:T(8,128)} %get-tuple-element.1028.gates, ...), custom_call_target="tpu_custom_call" | custom-call | flops 4831838208 | bytes 9437184 | tf_op jit(solution)/shard_map/cond/branch_1_fun/pallas_call | solution.py:244
  939.4 46.0 %collective-permute-done.42 = bf16[736,2048]{1,0:T(8,128)(2,1)} collective-permute-done((bf16[736,2048]{1,0:T(8,128)(2,1)}, bf16[736,2048]{1,0:T(8,128)(2,1)}, u32[]{:S(2)}, u32[]{:S(2)}) %collective-permute-start.42) | collective-permute-done | bytes 3014688 | tf_op jit(solution)/shard_map/cond/branch_1_fun/ppermute | solution.py:322
  985.3 5.9 add_convert_fusion.9.own
  991.2 11.7 branch_1_fun.17
  1003.0 6.1 broadcast.80
  1010.5 19.7 %collective-permute-done.31 = bf16[512,2048]{1,0:T(8,128)(2,1)} collective-permute-done((bf16[512,2048]{1,0:T(8,128)(2,1)S(1)}, bf16[512,2048]{1,0:T(8,128)(2,1)}, u32[]{:S(2)}, u32[]{:S(2)}) %collective-permute-start.31) | collective-permute-done | bytes 2097184 | tf_op jit(solution)/shard_map/cond/branch_1_fun/ppermute | solution.py:330
  1036.7 38.5 %collective-permute-done.35 = bf16[512,2048]{1,0:T(8,128)(2,1)} collective-permute-done((bf16[512,2048]{1,0:T(8,128)(2,1)}, bf16[512,2048]{1,0:T(8,128)(2,1)}, u32[]{:S(2)}, u32[]{:S(2)}) %collective-permute-start.35) | collective-permute-done | bytes 2097184 | tf_op jit(solution)/shard_map/cond/branch_1_fun/ppermute | solution.py:330
  1079.8 40.3 %collective-permute-done.41 = bf16[512,2048]{1,0:T(8,128)(2,1)} collective-permute-done((bf16[512,2048]{1,0:T(8,128)(2,1)}, bf16[512,2048]{1,0:T(8,128)(2,1)}, u32[]{:S(2)}, u32[]{:S(2)}) %collective-permute-start.41) | collective-permute-done | bytes 2097184 | tf_op jit(solution)/shard_map/cond/branch_1_fun/ppermute | solution.py:330
  1124.8 37.0 %collective-permute-done.45 = bf16[512,2048]{1,0:T(8,128)(2,1)} collective-permute-done((bf16[512,2048]{1,0:T(8,128)(2,1)}, bf16[512,2048]{1,0:T(8,128)(2,1)}, u32[]{:S(2)}, u32[]{:S(2)}) %collective-permute-start.45) | collective-permute-done | bytes 2097184 | tf_op jit(solution)/shard_map/cond/branch_1_fun/ppermute | solution.py:330
  (126 shorter events, 59.7 us)
Async XLA Ops:
  0.0 16.1 %copy-start = (bf16[2048,8]{0,1:T(8,128)(2,1)S(1)}, bf16[2048,8]{0,1:T(8,128)(2,1)}, u32[]{:S(2)}) copy-start(bf16[2048,8]{0,1:T(8,128)(2,1)} %param.16) | copy-start | bytes 98308
  52.4 119.9 %copy-start.27 = (f32[4096,2]{0,1:T(2,128)}, f32[4096,2]{0,1:T(2,128)S(1)}, u32[]{:S(2)}) copy-start(f32[4096,2]{0,1:T(2,128)S(1)} %get-tuple-element.579) | copy-start | bytes 98308 | tf_op jit(solution)/shard_map/cond
  52.4 119.9 %collective-permute-start.23 = (bf16[2,2048,2816]{2,1,0:T(8,128)(2,1)}, bf16[2,2048,2816]{2,1,0:T(8,128)(2,1)}, u32[]{:S(2)}, u32[]{:S(2)}) collective-permute-start(bf16[2,2048,2816]{2,1,0:T(8,128)(2,1)} %get-tuple-element.488.refs_4_.refs_2_), channel_id=1, source_target_pairs={{0,1},{1,0},{2,3},{3,2},{4,5},{5,4},{6,7},{7,6}} | collective-permute-start | bytes 69206024 | tf_op jit(solution)/shard_map/cond/branch_1_fun/ppermute | solution.py:311
  52.4 119.9 %collective-permute-start.24 = (bf16[2,2048,2816]{2,1,0:T(8,128)(2,1)}, bf16[2,2048,2816]{2,1,0:T(8,128)(2,1)}, u32[]{:S(2)}, u32[]{:S(2)}) collective-permute-start(bf16[2,2048,2816]{2,1,0:T(8,128)(2,1)} %get-tuple-element.493.refs_5_.refs_3_), channel_id=1, source_target_pairs={{0,1},{1,0},{2,3},{3,2},{4,5},{5,4},{6,7},{7,6}} | collective-permute-start | bytes 69206024 | tf_op jit(solution)/shard_map/cond/branch_1_fun/ppermute | solution.py:311
  52.9 121.4 %collective-permute-start.25 = (bf16[2,2816,2048]{2,1,0:T(8,128)(2,1)}, bf16[2,2816,2048]{2,1,0:T(8,128)(2,1)}, u32[]{:S(2)}, u32[]{:S(2)}) collective-permute-start(bf16[2,2816,2048]{2,1,0:T(8,128)(2,1)} %get-tuple-element.498.refs_6_.refs_4_), channel_id=1, source_target_pairs={{0,1},{1,0},{2,3},{3,2},{4,5},{5,4},{6,7},{7,6}} | collective-permute-start | bytes 69206024 | tf_op jit(solution)/shard_map/cond/branch_1_fun/ppermute | solution.py:311
  53.0 326.6 %collective-permute-start.27 = (bf16[1024,2048]{1,0:T(8,128)(2,1)}, bf16[1024,2048]{1,0:T(8,128)(2,1)}, u32[]{:S(2)}, u32[]{:S(2)}) collective-permute-start(bf16[1024,2048]{1,0:T(8,128)(2,1)} %get-tuple-element.215.refs_0_.refs_3_), channel_id=1, source_target_pairs={{0,2},{2,0},{1,3},{3,1},{4,6},{6,4},{5,7},{7,5}} | collective-permute-start | bytes 12582920 | tf_op jit(solution)/shard_map/cond/branch_1_fun/ppermute | solution.py:309
  54.5 325.1 %collective-permute-start.28 = (bf16[1024,2048]{1,0:T(8,128)(2,1)}, bf16[1024,2048]{1,0:T(8,128)(2,1)}, u32[]{:S(2)}, u32[]{:S(2)}) collective-permute-start(bf16[1024,2048]{1,0:T(8,128)(2,1)} %get-tuple-element.216.refs_1_.refs_4_), channel_id=1, source_target_pairs={{0,2},{2,0},{1,3},{3,1},{4,6},{6,4},{5,7},{7,5}} | collective-permute-start | bytes 12582920 | tf_op jit(solution)/shard_map/cond/branch_1_fun/ppermute | solution.py:309
  172.3 414.9 %collective-permute-start.37 = (bf16[1024,2048]{1,0:T(8,128)(2,1)}, bf16[1024,2048]{1,0:T(8,128)(2,1)}, u32[]{:S(2)}, u32[]{:S(2)}) collective-permute-start(bf16[1024,2048]{1,0:T(8,128)(2,1)} %get-tuple-element.217.refs_2_.refs_3_), channel_id=1, source_target_pairs={{0,2},{2,0},{1,3},{3,1},{4,6},{6,4},{5,7},{7,5}} | collective-permute-start | bytes 12582920 | tf_op jit(solution)/shard_map/cond/branch_1_fun/ppermute | solution.py:309
  172.3 414.9 %collective-permute-start.38 = (bf16[1024,2048]{1,0:T(8,128)(2,1)}, bf16[1024,2048]{1,0:T(8,128)(2,1)}, u32[]{:S(2)}, u32[]{:S(2)}) collective-permute-start(bf16[1024,2048]{1,0:T(8,128)(2,1)} %get-tuple-element.218.refs_3_.refs_4_), channel_id=1, source_target_pairs={{0,2},{2,0},{1,3},{3,1},{4,6},{6,4},{5,7},{7,5}} | collective-permute-start | bytes 12582920 | tf_op jit(solution)/shard_map/cond/branch_1_fun/ppermute | solution.py:309
  379.5 133.2 %copy-start.28 = (f32[4096,2]{0,1:T(2,128)S(1)}, f32[4096,2]{0,1:T(2,128)}, u32[]{:S(2)}) copy-start(f32[4096,2]{0,1:T(2,128)} %copy-done.27) | copy-start | bytes 98308 | tf_op jit(solution)/shard_map/cond
  379.5 133.2 %copy-start.62 = (f32[4096]{0:T(1024)S(1)}, f32[4096]{0:T(1024)}, u32[]{:S(2)}) copy-start(f32[4096]{0:T(1024)} %get-tuple-element.588) | copy-start | bytes 49156 | tf_op jit(solution)/shard_map/cond
  379.5 134.0 %copy-start.58 = (s32[4096,2]{0,1:T(2,128)S(1)}, s32[4096,2]{0,1:T(2,128)}, u32[]{:S(2)}) copy-start(s32[4096,2]{0,1:T(2,128)} %get-tuple-element.890) | copy-start | bytes 98308 | tf_op jit(solution)/shard_map/cond
  512.7 68.5 %collective-permute-start.29 = (bf16[736,2048]{1,0:T(8,128)(2,1)}, bf16[736,2048]{1,0:T(8,128)(2,1)}, u32[]{:S(2)}, u32[]{:S(2)}) collective-permute-start(bf16[736,2048]{1,0:T(8,128)(2,1)} %get-tuple-element.237), channel_id=1, source_target_pairs={{0,4},{4,0},{1,5},{5,1},{2,6},{6,2},{3,7},{7,3}} | collective-permute-start | bytes 9043976 | tf_op jit(solution)/shard_map/cond/branch_1_fun/ppermute | solution.py:322
  516.2 217.0 %collective-permute-start.26 = (bf16[736,2048]{1,0:T(8,128)(2,1)}, bf16[736,2048]{1,0:T(8,128)(2,1)}, u32[]{:S(2)}, u32[]{:S(2)}) collective-permute-start(bf16[736,2048]{1,0:T(8,128)(2,1)} %get-tuple-element.228), channel_id=1, source_target_pairs={{0,4},{4,0},{1,5},{5,1},{2,6},{6,2},{3,7},{7,3}} | collective-permute-start | bytes 9043976 | tf_op jit(solution)/shard_map/cond/branch_1_fun/ppermute | solution.py:322
  518.3 200.6 %collective-permute-start.33 = (bf16[736,2048]{1,0:T(8,128)(2,1)}, bf16[736,2048]{1,0:T(8,128)(2,1)}, u32[]{:S(2)}, u32[]{:S(2)}) collective-permute-start(bf16[736,2048]{1,0:T(8,128)(2,1)} %get-tuple-element.242), channel_id=1, source_target_pairs={{0,4},{4,0},{1,5},{5,1},{2,6},{6,2},{3,7},{7,3}} | collective-permute-start | bytes 9043976 | tf_op jit(solution)/shard_map/cond/branch_1_fun/ppermute | solution.py:322
  581.2 145.8 %collective-permute-start.32 = (bf16[736,2048]{1,0:T(8,128)(2,1)}, bf16[736,2048]{1,0:T(8,128)(2,1)}, u32[]{:S(2)}, u32[]{:S(2)}) collective-permute-start(bf16[736,2048]{1,0:T(8,128)(2,1)} %get-tuple-element.240), channel_id=1, source_target_pairs={{0,4},{4,0},{1,5},{5,1},{2,6},{6,2},{3,7},{7,3}} | collective-permute-start | bytes 9043976 | tf_op jit(solution)/shard_map/cond/branch_1_fun/ppermute | solution.py:322
  587.2 152.4 %collective-permute-start.30 = (bf16[736,2048]{1,0:T(8,128)(2,1)}, bf16[736,2048]{1,0:T(8,128)(2,1)}, u32[]{:S(2)}, u32[]{:S(2)}) collective-permute-start(bf16[736,2048]{1,0:T(8,128)(2,1)} %add_convert_fusion.14), channel_id=1, source_target_pairs={{0,2},{2,0},{1,3},{3,1},{4,6},{6,4},{5,7},{7,5}} | collective-permute-start | bytes 9043976 | tf_op jit(solution)/shard_map/cond/branch_1_fun/ppermute | solution.py:342
  716.9 74.6 %collective-permute-start.39 = (bf16[736,2048]{1,0:T(8,128)(2,1)}, bf16[736,2048]{1,0:T(8,128)(2,1)}, u32[]{:S(2)}, u32[]{:S(2)}) collective-permute-start(bf16[736,2048]{1,0:T(8,128)(2,1)} %get-tuple-element.246), channel_id=1, source_target_pairs={{0,4},{4,0},{1,5},{5,1},{2,6},{6,2},{3,7},{7,3}} | collective-permute-start | bytes 9043976 | tf_op jit(solution)/shard_map/cond/branch_1_fun/ppermute | solution.py:322
  724.9 71.3 %collective-permute-start.34 = (bf16[736,2048]{1,0:T(8,128)(2,1)}, bf16[736,2048]{1,0:T(8,128)(2,1)}, u32[]{:S(2)}, u32[]{:S(2)}) collective-permute-start(bf16[736,2048]{1,0:T(8,128)(2,1)} %add_convert_fusion.12), channel_id=1, source_target_pairs={{0,2},{2,0},{1,3},{3,1},{4,6},{6,4},{5,7},{7,5}} | collective-permute-start | bytes 9043976 | tf_op jit(solution)/shard_map/cond/branch_1_fun/ppermute | solution.py:342
  727.0 129.1 %collective-permute-start.43 = (bf16[736,2048]{1,0:T(8,128)(2,1)}, bf16[736,2048]{1,0:T(8,128)(2,1)}, u32[]{:S(2)}, u32[]{:S(2)}) collective-permute-start(bf16[736,2048]{1,0:T(8,128)(2,1)} %get-tuple-element.252), channel_id=1, source_target_pairs={{0,4},{4,0},{1,5},{5,1},{2,6},{6,2},{3,7},{7,3}} | collective-permute-start | bytes 9043976 | tf_op jit(solution)/shard_map/cond/branch_1_fun/ppermute | solution.py:322
  733.3 187.4 %collective-permute-start.36 = (bf16[736,2048]{1,0:T(8,128)(2,1)}, bf16[736,2048]{1,0:T(8,128)(2,1)}, u32[]{:S(2)}, u32[]{:S(2)}) collective-permute-start(bf16[736,2048]{1,0:T(8,128)(2,1)} %get-tuple-element.234), channel_id=1, source_target_pairs={{0,4},{4,0},{1,5},{5,1},{2,6},{6,2},{3,7},{7,3}} | collective-permute-start | bytes 9043976 | tf_op jit(solution)/shard_map/cond/branch_1_fun/ppermute | solution.py:322
  739.6 245.7 %collective-permute-start.42 = (bf16[736,2048]{1,0:T(8,128)(2,1)}, bf16[736,2048]{1,0:T(8,128)(2,1)}, u32[]{:S(2)}, u32[]{:S(2)}) collective-permute-start(bf16[736,2048]{1,0:T(8,128)(2,1)} %get-tuple-element.250), channel_id=1, source_target_pairs={{0,4},{4,0},{1,5},{5,1},{2,6},{6,2},{3,7},{7,3}} | collective-permute-start | bytes 9043976 | tf_op jit(solution)/shard_map/cond/branch_1_fun/ppermute | solution.py:322
  740.1 51.5 %copy-start.47 = (bf16[736,2048]{1,0:T(8,128)(2,1)S(1)}, bf16[736,2048]{1,0:T(8,128)(2,1)}, u32[]{:S(2)}) copy-start(bf16[736,2048]{1,0:T(8,128)(2,1)} %get-tuple-element.247) | copy-start | bytes 9043972 | tf_op jit(solution)/shard_map/cond
  796.2 129.2 %collective-permute-start.40 = (bf16[736,2048]{1,0:T(8,128)(2,1)}, bf16[736,2048]{1,0:T(8,128)(2,1)}, u32[]{:S(2)}, u32[]{:S(2)}) collective-permute-start(bf16[736,2048]{1,0:T(8,128)(2,1)} %add_convert_fusion.10), channel_id=1, source_target_pairs={{0,2},{2,0},{1,3},{3,1},{4,6},{6,4},{5,7},{7,5}} | collective-permute-start | bytes 9043976 | tf_op jit(solution)/shard_map/cond/branch_1_fun/ppermute | solution.py:346
  856.1 64.6 %copy-start.48 = (bf16[736,2048]{1,0:T(8,128)(2,1)S(1)}, bf16[736,2048]{1,0:T(8,128)(2,1)}, u32[]{:S(2)}) copy-start(bf16[736,2048]{1,0:T(8,128)(2,1)} %get-tuple-element.243) | copy-start | bytes 9043972 | tf_op jit(solution)/shard_map/cond
  862.2 129.0 %collective-permute-start.44 = (bf16[736,2048]{1,0:T(8,128)(2,1)}, bf16[736,2048]{1,0:T(8,128)(2,1)}, u32[]{:S(2)}, u32[]{:S(2)}) collective-permute-start(bf16[736,2048]{1,0:T(8,128)(2,1)} %add_convert_fusion.8), channel_id=1, source_target_pairs={{0,2},{2,0},{1,3},{3,1},{4,6},{6,4},{5,7},{7,5}} | collective-permute-start | bytes 9043976 | tf_op jit(solution)/shard_map/cond/branch_1_fun/ppermute | solution.py:346
  862.2 168.1 %collective-permute-start.31 = (bf16[512,2048]{1,0:T(8,128)(2,1)S(1)}, bf16[512,2048]{1,0:T(8,128)(2,1)}, u32[]{:S(2)}, u32[]{:S(2)}) collective-permute-start(bf16[512,2048]{1,0:T(8,128)(2,1)S(1)} %copy-done.10), channel_id=1, source_target_pairs={{0,4},{4,0},{1,5},{5,1},{2,6},{6,2},{3,7},{7,3}} | collective-permute-start | bytes 6291464 | tf_op jit(solution)/shard_map/cond/branch_1_fun/ppermute | solution.py:330
  925.5 149.7 %collective-permute-start.35 = (bf16[512,2048]{1,0:T(8,128)(2,1)}, bf16[512,2048]{1,0:T(8,128)(2,1)}, u32[]{:S(2)}, u32[]{:S(2)}) collective-permute-start(bf16[512,2048]{1,0:T(8,128)(2,1)} %branch_1_fun.14), channel_id=1, source_target_pairs={{0,4},{4,0},{1,5},{5,1},{2,6},{6,2},{3,7},{7,3}} | collective-permute-start | bytes 6291464 | tf_op jit(solution)/shard_map/cond/branch_1_fun/ppermute | solution.py:330
  937.4 182.8 %collective-permute-start.41 = (bf16[512,2048]{1,0:T(8,128)(2,1)}, bf16[512,2048]{1,0:T(8,128)(2,1)}, u32[]{:S(2)}, u32[]{:S(2)}) collective-permute-start(bf16[512,2048]{1,0:T(8,128)(2,1)} %branch_1_fun.16), channel_id=1, source_target_pairs={{0,4},{4,0},{1,5},{5,1},{2,6},{6,2},{3,7},{7,3}} | collective-permute-start | bytes 6291464 | tf_op jit(solution)/shard_map/cond/branch_1_fun/ppermute | solution.py:330
  1002.9 158.8 %collective-permute-start.45 = (bf16[512,2048]{1,0:T(8,128)(2,1)}, bf16[512,2048]{1,0:T(8,128)(2,1)}, u32[]{:S(2)}, u32[]{:S(2)}) collective-permute-start(bf16[512,2048]{1,0:T(8,128)(2,1)} %branch_1_fun.17), channel_id=1, source_target_pairs={{0,4},{4,0},{1,5},{5,1},{2,6},{6,2},{3,7},{7,3}} | collective-permute-start | bytes 6291464 | tf_op jit(solution)/shard_map/cond/branch_1_fun/ppermute | solution.py:330
  1033.4 44.9 %copy-start.14 = (bf16[512,2048]{1,0:T(8,128)(2,1)S(1)}, bf16[512,2048]{1,0:T(8,128)(2,1)}, u32[]{:S(2)}) copy-start(bf16[512,2048]{1,0:T(8,128)(2,1)} %branch_1_fun.16) | copy-start | bytes 6291460 | tf_op jit(solution)/shard_map/cond
  1078.4 44.9 %copy-start.18 = (bf16[512,2048]{1,0:T(8,128)(2,1)S(1)}, bf16[512,2048]{1,0:T(8,128)(2,1)}, u32[]{:S(2)}) copy-start(bf16[512,2048]{1,0:T(8,128)(2,1)} %branch_1_fun.17) | copy-start | bytes 6291460 | tf_op jit(solution)/shard_map/cond
  (11 other events, 55.8 us)
where the time goes:
time: 1180 us
  Pallas kernels  636 us (54%)
  waiting for transfers between devices  391 us (33%)
  other arithmetic  59.4 us (5%)
  local copies, waits for them, and re-layouts  40.3 us (3%)
  loops' own time  18.1 us (2%)
  starting transfers between devices  12.8 us (1%)
    pallas_call x5, Pallas kernels, run_ffn(): pl.pallas_call(kern, out_shape=[jax.ShapeDtypeStruct((cap, dim), jnp.bflo...  585 us
    ppermute x8, waiting for transfers between devices, swap_tp(): return lax.ppermute(send, 'tp', [(0, 1), (1, 0)])  255 us
    ppermute x4, waiting for transfers between devices, mix(): pieces.append((piece, lax.ppermute(piece, 'tp', [(0, 1), (1, 0)])))  136 us
    pallas_call x4, Pallas kernels, run_mix(): pl.pallas_call(functools.partial(mix_kernel, quarter), out_shape=jax.Shap...  47.3 us
    convert_element_type x6, other arithmetic, reduce(): (keep.astype(jnp.float32) + got.astype(jnp.float32)).astype(jnp.bfloat16)  32.2 us
  transfers between devices with their start and end apart: 23, of which 9 were waited for; matrix products, arithmetic and copies ran while one was open for 6% of the time, Pallas kernels for 54%

commit v1 on v0

--- a/solution.py
+++ b/solution.py
@@ -33,7 +33,9 @@
 def ffn_kernel(rel, q0, n, groups, pos_ref, cnt_ref, rank_ref, *refs):
     ng = len(groups)
     toks, ws = refs[:n], [refs[n + 3 * i:n + 3 * i + 3] for i in range(ng)]
-    outs, (tokb, hbuf, acc, b1, b3, b2, tsem, wsem, osem) = refs[-9 - 2 * n:-9], refs[-9:]
+    outs, (tokb, hbuf, stage, acc, b1, b3, b2, tsem, wsem, osem) = refs[-10 - 2 * n:-10], refs[-10:]
+    apart = n <= 2
+    stage = stage if apart else hbuf
     me, half = pos_ref[0], pos_ref[1]
     block = me ^ rel
     nf = ws[0][0].shape[2] // FCH
@@ -85,19 +87,15 @@
         total = lax.fori_loop(0, 2 * n, piece, jnp.int32(0))
         half_tile = TILE // 2
         nt = (total + half_tile - 1) // TILE
-        rest = total > nt * TILE
+        rest = total - nt * TILE
 
         def tile(j, rows=TILE):
             return pl.ds(pl.multiple_of(j * TILE, TILE), rows)
 
         def over_tiles(do):
             pl.loop(0, nt)(lambda j: do(tile(j)))
-            pl.when(rest)(lambda: do(tile(nt, half_tile)))
-
-        def clear(at):
-            acc[at, :] = jnp.zeros((at.size, acc.shape[1]), jnp.float32)
-
-        over_tiles(clear)
+            pl.when(rest > half_tile // 2)(lambda: do(tile(nt, half_tile)))
+            pl.when((rest > 0) & (rest <= half_tile // 2))(lambda: do(tile(nt, half_tile // 2)))
 
         def width(f, _):
             g = e * nf + f
@@ -112,35 +110,44 @@
                 a = jnp.dot(h, b1[s], preferred_element_type=jnp.float32)
                 b = jnp.dot(h, b3[s], preferred_element_type=jnp.float32)
                 u = (jax.nn.silu(a) * b).astype(jnp.bfloat16)
-                acc[at, :] += jnp.dot(u, b2[s], preferred_element_type=jnp.float32)
+                before = jnp.where(f > 0, acc[at, :], 0.0)
+                acc[at, :] = before + jnp.dot(u, b2[s], preferred_element_type=jnp.float32)
 
             over_tiles(rows)
             return 0
 
         lax.fori_loop(0, nf, width, 0)
 
+        @pl.when((e > 0) & apart)
+        def _():
+            move(e - 1, bases, True)
+
         def cast(at):
-            hbuf[at, :] = acc[at, :].astype(jnp.bfloat16)
+            stage[at, :] = acc[at, :].astype(jnp.bfloat16)
 
         over_tiles(cast)
+        ends = move(e, bases, False)
+        if not apart:
+            move(e, ends, True)
+        return ends
+
+    def move(e, bases, wait):
+        exp = 2 * (me ^ (groups[0] + e // 2)) + e % 2
         ends, lo = [], jnp.int32(0)
-        places = []
         for p in range(2 * n):
             size = padded(count_at(cnt_ref, block, exp, q0 + p % n, 1 - half if p < n else half))
-            places.append((outs[p], bases[p], lo, size))
-            ends.append(bases[p] + size)
+            base = bases[p] - size if wait else bases[p]
+            whole = size // SUB
+
+            def copy(at, rows):
+                c = pltpu.make_async_copy(stage.at[pl.ds(pl.multiple_of(lo + at, ALIGN), rows)],
+                                          outs[p].at[pl.ds(pl.multiple_of(base + at, ALIGN), rows)], osem)
+                c.wait() if wait else c.start()
+
+            pl.loop(0, whole)(lambda j: copy(j * SUB, SUB))
+            pl.loop(0, (size - whole * SUB) // ALIGN)(lambda j: copy(whole * SUB + j * ALIGN, ALIGN))
+            ends.append(base + size)
             lo += size
-        for wait in (False, True):
-            for dst, base, lo, size in places:
-                whole = size // SUB
-
-                def copy(at, rows):
-                    c = pltpu.make_async_copy(hbuf.at[pl.ds(pl.multiple_of(lo + at, ALIGN), rows)],
-                                              dst.at[pl.ds(pl.multiple_of(base + at, ALIGN), rows)], osem)
-                    c.wait() if wait else c.start()
-
-                pl.loop(0, whole)(lambda j: copy(j * SUB, SUB))
-                pl.loop(0, (size - whole * SUB) // ALIGN)(lambda j: copy(whole * SUB + j * ALIGN, ALIGN))
         return tuple(ends)
 
     start = []
@@ -150,7 +157,9 @@
             for e in range(2):
                 at += padded(count_at(cnt_ref, block, 2 * me + e, q0 + p % n, 1 - half if p < n else half))
         start.append(at)
-    lax.fori_loop(0, 2 * ng, expert, tuple(start))
+    ends = lax.fori_loop(0, 2 * ng, expert, tuple(start))
+    if apart:
+        move(jnp.int32(2 * ng - 1), ends, True)
 
 
 def run_ffn(rel, q0, n, groups, cap, pos, cnt, ranks, toks, weights, into=()):
@@ -171,6 +180,7 @@
         scratch_shapes=[
             pltpu.VMEM((n * 2 * PIECE, dim), jnp.bfloat16),
             pltpu.VMEM((RP, dim), jnp.bfloat16),
+            pltpu.VMEM((RP if n <= 2 else ALIGN, dim), jnp.bfloat16),
             pltpu.VMEM((RP, dim), jnp.float32),
             pltpu.VMEM((2, dim, FCH), jnp.bfloat16),
             pltpu.VMEM((2, dim, FCH), jnp.bfloat16),

time: 1180 us -> 1170 us (level)
  Pallas kernels: 636 us -> 616 us
    ppermute x8, waiting for transfers between devices: 255 us -> 279 us  [swap_tp(): return lax.ppermute(send, 'tp', [(0, 1), (1, 0)])]
    pallas_call x5, Pallas kernels: 585 us -> 564 us  [run_ffn(): pl.pallas_call(kern, out_shape=[jax.ShapeDtypeStruct((cap, dim), jnp.bflo...]
    ppermute x4, waiting for transfers between devices: 136 us -> 122 us  [mix(): pieces.append((piece, lax.ppermute(piece, 'tp', [(0, 1), (1, 0)])))]
  transfers between devices with their start and end apart: 23 -> 23, of which waited for: 9 -> 10; matrix products, arithmetic and copies ran while one was open for 6% -> 6% of each run, Pallas kernels for 54% -> 53%
where the time goes in v1:
time: 1170 us; the launch traced here: 1160 us
  Pallas kernels  616 us (53%)
  waiting for transfers between devices  402 us (34%)
  other arithmetic  59.4 us (5%)
  local copies, waits for them, and re-layouts  39.9 us (3%)
  loops' own time  14.3 us (1%)
  starting transfers between devices  12.8 us (1%)
    pallas_call x5, Pallas kernels, run_ffn(): pl.pallas_call(kern, out_shape=[jax.ShapeDtypeStruct((cap, dim), jnp.bflo...  564 us
    ppermute x8, waiting for transfers between devices, swap_tp(): return lax.ppermute(send, 'tp', [(0, 1), (1, 0)])  279 us
    ppermute x4, waiting for transfers between devices, mix(): pieces.append((piece, lax.ppermute(piece, 'tp', [(0, 1), (1, 0)])))  122 us
    pallas_call x4, Pallas kernels, run_mix(): pl.pallas_call(functools.partial(mix_kernel, quarter), out_shape=jax.Shap...  48 us
    convert_element_type x6, other arithmetic, reduce(): (keep.astype(jnp.float32) + got.astype(jnp.float32)).astype(jnp.bfloat16)  32.2 us
  transfers between devices with their start and end apart: 23, of which 10 were waited for; matrix products, arithmetic and copies ran while one was open for 6% of the time, Pallas kernels for 53%

profile of v1, /device:TPU:6, one launch (start us, length us, event | category | flops | bytes accessed | tf_op | source)
XLA Modules:
  0.0 1162.2 jit_solution(1000380066963435322)
XLA Ops:
  0.0 7.7 fusion.15
  10.6 5.5 fusion.17
  27.0 7.5 all-gather.1
  43.9 1117.2 %conditional.1 = (bf16[4096,2048]{1,0:T(8,128)(2,1)}) conditional(s32[]{:T(128)} %bitcast.77, (s32[4096,8]{1,0:T(8,128)}, s32[4096,2]{0,1:T(2,128)}, f32[4096,2]{0,1:T(2,128)S(1)}, s32[2]{0:T(128)S(1)}, s32[256]{0:T(256)S(1)}, /*index=5*/pred[64,512]{1,0:T(32,128)(4,1)S(1)}, bf16[1024,2048]{1,0:T(8,128)(2,1)}, ...), branch_computations={%region_9.10_spmd, %region_10.11_spmd, %region_11.12_spmd, %region... | conditional | flops 302866563072 | bytes 1342292480 | solution.py:373
  53.8 115.1 %branch_1_fun.9 = (bf16[736,2048]{1,0:T(8,128)(2,1)}, bf16[736,2048]{1,0:T(8,128)(2,1)}, bf16[736,2048]{1,0:T(8,128)(2,1)}, bf16[736,2048]{1,0:T(8,128)(2,1)}, b...) custom-call(s32[2]{0:T(128)S(1)} %get-tuple-element.244.pos_ref.refs, ...), custom_call_target="tpu_custom_call" | custom-call | flops 70866960384 | bytes 69206016 | tf_op jit(solution)/shard_map/cond/branch_1_fun/pallas_call | solution.py:174
  171.0 99.7 %branch_1_fun.10 = (bf16[736,2048]{1,0:T(8,128)(2,1)}, bf16[736,2048]{1,0:T(8,128)(2,1)}, bf16[736,2048]{1,0:T(8,128)(2,1)}, bf16[736,2048]{1,0:T(8,128)(2,1)}) custom-call(s32[2]{0:T(128)S(1)} %get-tuple-element.244.pos_ref.refs_0_, ...), custom_call_target="tpu_custom_call", output_to_operand_aliasing={{0}: (8, {}), {1}: (9, {}), {2}: (10, {}), {3}: (11, {})} | custom-call | flops 35433480192 | bytes 69206016 | tf_op jit(solution)/shard_map/cond/branch_1_fun/pallas_call | solution.py:174
  270.7 98.9 %branch_1_fun.11 = (bf16[736,2048]{1,0:T(8,128)(2,1)}, bf16[736,2048]{1,0:T(8,128)(2,1)}, bf16[736,2048]{1,0:T(8,128)(2,1)}, bf16[736,2048]{1,0:T(8,128)(2,1)}) custom-call(s32[2]{0:T(128)S(1)} %get-tuple-element.244.pos_ref.refs_0_, ...), custom_call_target="tpu_custom_call", output_to_operand_aliasing={{0}: (8, {}), {1}: (9, {}), {2}: (10, {}), {3}: (11, {})} | custom-call | flops 35433480192 | bytes 69206016 | tf_op jit(solution)/shard_map/cond/branch_1_fun/pallas_call | solution.py:174
  369.7 127.1 %branch_1_fun.12 = (bf16[736,2048]{1,0:T(8,128)(2,1)}, bf16[736,2048]{1,0:T(8,128)(2,1)}, bf16[736,2048]{1,0:T(8,128)(2,1)}, bf16[736,2048]{1,0:T(8,128)(2,1)}) custom-call(s32[2]{0:T(128)S(1)} %get-tuple-element.244.pos_ref.refs_0_, s32[256]{0:T(256)S(1)} %get-tuple-element.209.cnt_ref.refs_1_, s32[64,512]{1,0:T(8,128)} %select_n.148.rank_ref.refs_2_, ...), custom_call_target="tpu_custom_call" | custom-call | flops 70866960384 | bytes 138412032 | tf_op jit(solution)/shard_map/cond/branch_1_fun/pallas_call | solution.py:174
  502.4 62.9 %collective-permute-done.29 = bf16[736,2048]{1,0:T(8,128)(2,1)} collective-permute-done((bf16[736,2048]{1,0:T(8,128)(2,1)}, bf16[736,2048]{1,0:T(8,128)(2,1)}, u32[]{:S(2)}, u32[]{:S(2)}) %collective-permute-start.29) | collective-permute-done | bytes 3014688 | tf_op jit(solution)/shard_map/cond/branch_1_fun/ppermute | solution.py:332
  565.3 6.0 add_convert_fusion.14
  571.3 122.9 %branch_1_fun.15 = (bf16[736,2048]{1,0:T(8,128)(2,1)}, bf16[736,2048]{1,0:T(8,128)(2,1)}, bf16[736,2048]{1,0:T(8,128)(2,1)}, bf16[736,2048]{1,0:T(8,128)(2,1)}) custom-call(s32[2]{0:T(128)S(1)} %get-tuple-element.244.pos_ref.refs_0_, s32[256]{0:T(256)S(1)} %get-tuple-element.209.cnt_ref.refs_1_, s32[64,512]{1,0:T(8,128)} %select_n.148.rank_ref.refs_2_, ...), custom_call_target="tpu_custom_call" | custom-call | flops 70866960384 | bytes 138412032 | tf_op jit(solution)/shard_map/cond/branch_1_fun/pallas_call | solution.py:174
  696.2 6.0 add_convert_fusion.12
  704.2 24.5 %collective-permute-done.32 = bf16[736,2048]{1,0:T(8,128)(2,1)} collective-permute-done((bf16[736,2048]{1,0:T(8,128)(2,1)}, bf16[736,2048]{1,0:T(8,128)(2,1)}, u32[]{:S(2)}, u32[]{:S(2)}) %collective-permute-start.32) | collective-permute-done | bytes 3014688 | tf_op jit(solution)/shard_map/cond/branch_1_fun/ppermute | solution.py:332
  729.8 4.9 add_convert_fusion.13.own
  736.7 4.7 add_convert_fusion.15.own
  741.4 12.1 %branch_1_fun.13 = bf16[512,2048]{1,0:T(8,128)(2,1)} custom-call(s32[2]{0:T(128)S(1)} %get-tuple-element.244.pos_ref.refs_0_, s32[256]{0:T(256)S(1)} %get-tuple-element.209.cnt_ref.refs_1_, s32[512,8]{1,0:T(8,128)} %get-tuple-element.1024.ranks, s32[512,2]{1,0:T(8,128)} %get-tuple-element.1020.ids, f32[512,2]{1,0:T(8,128)} %get-tuple-element.1027.gates, ...), custom_call_target="tpu_custom_call" | custom-call | flops 4831838208 | bytes 9437184 | tf_op jit(solution)/shard_map/cond/branch_1_fun/pallas_call | solution.py:254
  753.6 39.8 %collective-permute-done.39 = bf16[736,2048]{1,0:T(8,128)(2,1)} collective-permute-done((bf16[736,2048]{1,0:T(8,128)(2,1)}, bf16[736,2048]{1,0:T(8,128)(2,1)}, u32[]{:S(2)}, u32[]{:S(2)}) %collective-permute-start.39) | collective-permute-done | bytes 3014688 | tf_op jit(solution)/shard_map/cond/branch_1_fun/ppermute | solution.py:332
  793.4 4.7 add_convert_fusion.10
  798.1 11.9 %branch_1_fun.14 = bf16[512,2048]{1,0:T(8,128)(2,1)} custom-call(s32[2]{0:T(128)S(1)} %get-tuple-element.244.pos_ref.refs_0_, s32[256]{0:T(256)S(1)} %get-tuple-element.209.cnt_ref.refs_1_, s32[512,8]{1,0:T(8,128)} %get-tuple-element.1023.ranks, s32[512,2]{1,0:T(8,128)} %get-tuple-element.1019.ids, f32[512,2]{1,0:T(8,128)} %get-tuple-element.1026.gates, ...), custom_call_target="tpu_custom_call" | custom-call | flops 4831838208 | bytes 9437184 | tf_op jit(solution)/shard_map/cond/branch_1_fun/pallas_call | solution.py:254
  810.0 48.0 %collective-permute-done.43 = bf16[736,2048]{1,0:T(8,128)(2,1)} collective-permute-done((bf16[736,2048]{1,0:T(8,128)(2,1)}, bf16[736,2048]{1,0:T(8,128)(2,1)}, u32[]{:S(2)}, u32[]{:S(2)}) %collective-permute-start.43) | collective-permute-done | bytes 3014688 | tf_op jit(solution)/shard_map/cond/branch_1_fun/ppermute | solution.py:332
  858.0 6.1 add_convert_fusion.8
  864.0 58.5 %collective-permute-done.36 = bf16[736,2048]{1,0:T(8,128)(2,1)} collective-permute-done((bf16[736,2048]{1,0:T(8,128)(2,1)}, bf16[736,2048]{1,0:T(8,128)(2,1)}, u32[]{:S(2)}, u32[]{:S(2)}) %collective-permute-start.36) | collective-permute-done | bytes 3014688 | tf_op jit(solution)/shard_map/cond/branch_1_fun/ppermute | solution.py:332
  922.6 4.7 add_convert_fusion.11.own
  927.3 12.1 %branch_1_fun.16 = bf16[512,2048]{1,0:T(8,128)(2,1)} custom-call(s32[2]{0:T(128)S(1)} %get-tuple-element.244.pos_ref.refs_0_, s32[256]{0:T(256)S(1)} %get-tuple-element.209.cnt_ref.refs_1_, s32[512,8]{1,0:T(8,128)} %get-tuple-element.1022.ranks, s32[512,2]{1,0:T(8,128)} %get-tuple-element.1018.ids, f32[512,2]{1,0:T(8,128)} %get-tuple-element.1028.gates, ...), custom_call_target="tpu_custom_call" | custom-call | flops 4831838208 | bytes 9437184 | tf_op jit(solution)/shard_map/cond/branch_1_fun/pallas_call | solution.py:254
  941.5 45.7 %collective-permute-done.42 = bf16[736,2048]{1,0:T(8,128)(2,1)} collective-permute-done((bf16[736,2048]{1,0:T(8,128)(2,1)}, bf16[736,2048]{1,0:T(8,128)(2,1)}, u32[]{:S(2)}, u32[]{:S(2)}) %collective-permute-start.42) | collective-permute-done | bytes 3014688 | tf_op jit(solution)/shard_map/cond/branch_1_fun/ppermute | solution.py:332
  987.2 5.9 add_convert_fusion.9.own
  993.1 11.9 %branch_1_fun.17 = bf16[512,2048]{1,0:T(8,128)(2,1)} custom-call(s32[2]{0:T(128)S(1)} %get-tuple-element.244.pos_ref.refs_0_, s32[256]{0:T(256)S(1)} %get-tuple-element.209.cnt_ref.refs_1_, s32[512,8]{1,0:T(8,128)} %get-tuple-element.1021.ranks, s32[512,2]{1,0:T(8,128)} %get-tuple-element.1017.ids, f32[512,2]{1,0:T(8,128)} %get-tuple-element.1025.gates, ...), custom_call_target="tpu_custom_call" | custom-call | flops 4831838208 | bytes 9437184 | tf_op jit(solution)/shard_map/cond/branch_1_fun/pallas_call | solution.py:254
  1005.0 6.1 broadcast.80
  1012.5 19.6 %collective-permute-done.31 = bf16[512,2048]{1,0:T(8,128)(2,1)} collective-permute-done((bf16[512,2048]{1,0:T(8,128)(2,1)S(1)}, bf16[512,2048]{1,0:T(8,128)(2,1)}, u32[]{:S(2)}, u32[]{:S(2)}) %collective-permute-start.31) | collective-permute-done | bytes 2097184 | tf_op jit(solution)/shard_map/cond/branch_1_fun/ppermute | solution.py:340
  1038.6 38.5 %collective-permute-done.35 = bf16[512,2048]{1,0:T(8,128)(2,1)} collective-permute-done((bf16[512,2048]{1,0:T(8,128)(2,1)}, bf16[512,2048]{1,0:T(8,128)(2,1)}, u32[]{:S(2)}, u32[]{:S(2)}) %collective-permute-start.35) | collective-permute-done | bytes 2097184 | tf_op jit(solution)/shard_map/cond/branch_1_fun/ppermute | solution.py:340
  1081.7 40.3 %collective-permute-done.41 = bf16[512,2048]{1,0:T(8,128)(2,1)} collective-permute-done((bf16[512,2048]{1,0:T(8,128)(2,1)}, bf16[512,2048]{1,0:T(8,128)(2,1)}, u32[]{:S(2)}, u32[]{:S(2)}) %collective-permute-start.41) | collective-permute-done | bytes 2097184 | tf_op jit(solution)/shard_map/cond/branch_1_fun/ppermute | solution.py:340
  1126.6 24.0 %collective-permute-done.45 = bf16[512,2048]{1,0:T(8,128)(2,1)} collective-permute-done((bf16[512,2048]{1,0:T(8,128)(2,1)}, bf16[512,2048]{1,0:T(8,128)(2,1)}, u32[]{:S(2)}, u32[]{:S(2)}) %collective-permute-start.45) | collective-permute-done | bytes 2097184 | tf_op jit(solution)/shard_map/cond/branch_1_fun/ppermute | solution.py:340
  (126 shorter events, 63.5 us)
Async XLA Ops:
  50.5 118.4 %copy-start.27 = (f32[4096,2]{0,1:T(2,128)}, f32[4096,2]{0,1:T(2,128)S(1)}, u32[]{:S(2)}) copy-start(f32[4096,2]{0,1:T(2,128)S(1)} %get-tuple-element.579) | copy-start | bytes 98308 | tf_op jit(solution)/shard_map/cond
  50.5 118.4 %collective-permute-start.23 = (bf16[2,2048,2816]{2,1,0:T(8,128)(2,1)}, bf16[2,2048,2816]{2,1,0:T(8,128)(2,1)}, u32[]{:S(2)}, u32[]{:S(2)}) collective-permute-start(bf16[2,2048,2816]{2,1,0:T(8,128)(2,1)} %get-tuple-element.488.refs_4_.refs_2_), channel_id=1, source_target_pairs={{0,1},{1,0},{2,3},{3,2},{4,5},{5,4},{6,7},{7,6}} | collective-permute-start | bytes 69206024 | tf_op jit(solution)/shard_map/cond/branch_1_fun/ppermute | solution.py:321
  50.6 118.4 %collective-permute-start.24 = (bf16[2,2048,2816]{2,1,0:T(8,128)(2,1)}, bf16[2,2048,2816]{2,1,0:T(8,128)(2,1)}, u32[]{:S(2)}, u32[]{:S(2)}) collective-permute-start(bf16[2,2048,2816]{2,1,0:T(8,128)(2,1)} %get-tuple-element.493.refs_5_.refs_3_), channel_id=1, source_target_pairs={{0,1},{1,0},{2,3},{3,2},{4,5},{5,4},{6,7},{7,6}} | collective-permute-start | bytes 69206024 | tf_op jit(solution)/shard_map/cond/branch_1_fun/ppermute | solution.py:321
  51.1 119.9 %collective-permute-start.25 = (bf16[2,2816,2048]{2,1,0:T(8,128)(2,1)}, bf16[2,2816,2048]{2,1,0:T(8,128)(2,1)}, u32[]{:S(2)}, u32[]{:S(2)}) collective-permute-start(bf16[2,2816,2048]{2,1,0:T(8,128)(2,1)} %get-tuple-element.498.refs_6_.refs_4_), channel_id=1, source_target_pairs={{0,1},{1,0},{2,3},{3,2},{4,5},{5,4},{6,7},{7,6}} | collective-permute-start | bytes 69206024 | tf_op jit(solution)/shard_map/cond/branch_1_fun/ppermute | solution.py:321
  51.1 318.5 %collective-permute-start.27 = (bf16[1024,2048]{1,0:T(8,128)(2,1)}, bf16[1024,2048]{1,0:T(8,128)(2,1)}, u32[]{:S(2)}, u32[]{:S(2)}) collective-permute-start(bf16[1024,2048]{1,0:T(8,128)(2,1)} %get-tuple-element.215.refs_0_.refs_3_), channel_id=1, source_target_pairs={{0,2},{2,0},{1,3},{3,1},{4,6},{6,4},{5,7},{7,5}} | collective-permute-start | bytes 12582920 | tf_op jit(solution)/shard_map/cond/branch_1_fun/ppermute | solution.py:319
  52.6 317.1 %collective-permute-start.28 = (bf16[1024,2048]{1,0:T(8,128)(2,1)}, bf16[1024,2048]{1,0:T(8,128)(2,1)}, u32[]{:S(2)}, u32[]{:S(2)}) collective-permute-start(bf16[1024,2048]{1,0:T(8,128)(2,1)} %get-tuple-element.216.refs_1_.refs_4_), channel_id=1, source_target_pairs={{0,2},{2,0},{1,3},{3,1},{4,6},{6,4},{5,7},{7,5}} | collective-permute-start | bytes 12582920 | tf_op jit(solution)/shard_map/cond/branch_1_fun/ppermute | solution.py:319
  169.0 402.3 %collective-permute-start.37 = (bf16[1024,2048]{1,0:T(8,128)(2,1)}, bf16[1024,2048]{1,0:T(8,128)(2,1)}, u32[]{:S(2)}, u32[]{:S(2)}) collective-permute-start(bf16[1024,2048]{1,0:T(8,128)(2,1)} %get-tuple-element.217.refs_2_.refs_3_), channel_id=1, source_target_pairs={{0,2},{2,0},{1,3},{3,1},{4,6},{6,4},{5,7},{7,5}} | collective-permute-start | bytes 12582920 | tf_op jit(solution)/shard_map/cond/branch_1_fun/ppermute | solution.py:319
  169.0 402.3 %collective-permute-start.38 = (bf16[1024,2048]{1,0:T(8,128)(2,1)}, bf16[1024,2048]{1,0:T(8,128)(2,1)}, u32[]{:S(2)}, u32[]{:S(2)}) collective-permute-start(bf16[1024,2048]{1,0:T(8,128)(2,1)} %get-tuple-element.218.refs_3_.refs_4_), channel_id=1, source_target_pairs={{0,2},{2,0},{1,3},{3,1},{4,6},{6,4},{5,7},{7,5}} | collective-permute-start | bytes 12582920 | tf_op jit(solution)/shard_map/cond/branch_1_fun/ppermute | solution.py:319
  369.6 127.2 %copy-start.28 = (f32[4096,2]{0,1:T(2,128)S(1)}, f32[4096,2]{0,1:T(2,128)}, u32[]{:S(2)}) copy-start(f32[4096,2]{0,1:T(2,128)} %copy-done.27) | copy-start | bytes 98308 | tf_op jit(solution)/shard_map/cond
  369.6 127.2 %copy-start.62 = (f32[4096]{0:T(1024)S(1)}, f32[4096]{0:T(1024)}, u32[]{:S(2)}) copy-start(f32[4096]{0:T(1024)} %get-tuple-element.588) | copy-start | bytes 49156 | tf_op jit(solution)/shard_map/cond
  369.6 127.9 %copy-start.58 = (s32[4096,2]{0,1:T(2,128)S(1)}, s32[4096,2]{0,1:T(2,128)}, u32[]{:S(2)}) copy-start(s32[4096,2]{0,1:T(2,128)} %get-tuple-element.890) | copy-start | bytes 98308 | tf_op jit(solution)/shard_map/cond
  496.8 68.5 %collective-permute-start.29 = (bf16[736,2048]{1,0:T(8,128)(2,1)}, bf16[736,2048]{1,0:T(8,128)(2,1)}, u32[]{:S(2)}, u32[]{:S(2)}) collective-permute-start(bf16[736,2048]{1,0:T(8,128)(2,1)} %get-tuple-element.237), channel_id=1, source_target_pairs={{0,4},{4,0},{1,5},{5,1},{2,6},{6,2},{3,7},{7,3}} | collective-permute-start | bytes 9043976 | tf_op jit(solution)/shard_map/cond/branch_1_fun/ppermute | solution.py:332
  500.3 234.3 %collective-permute-start.26 = (bf16[736,2048]{1,0:T(8,128)(2,1)}, bf16[736,2048]{1,0:T(8,128)(2,1)}, u32[]{:S(2)}, u32[]{:S(2)}) collective-permute-start(bf16[736,2048]{1,0:T(8,128)(2,1)} %get-tuple-element.228), channel_id=1, source_target_pairs={{0,4},{4,0},{1,5},{5,1},{2,6},{6,2},{3,7},{7,3}} | collective-permute-start | bytes 9043976 | tf_op jit(solution)/shard_map/cond/branch_1_fun/ppermute | solution.py:332
  502.3 193.8 %collective-permute-start.33 = (bf16[736,2048]{1,0:T(8,128)(2,1)}, bf16[736,2048]{1,0:T(8,128)(2,1)}, u32[]{:S(2)}, u32[]{:S(2)}) collective-permute-start(bf16[736,2048]{1,0:T(8,128)(2,1)} %get-tuple-element.242), channel_id=1, source_target_pairs={{0,4},{4,0},{1,5},{5,1},{2,6},{6,2},{3,7},{7,3}} | collective-permute-start | bytes 9043976 | tf_op jit(solution)/shard_map/cond/branch_1_fun/ppermute | solution.py:332
  565.3 163.5 %collective-permute-start.32 = (bf16[736,2048]{1,0:T(8,128)(2,1)}, bf16[736,2048]{1,0:T(8,128)(2,1)}, u32[]{:S(2)}, u32[]{:S(2)}) collective-permute-start(bf16[736,2048]{1,0:T(8,128)(2,1)} %get-tuple-element.240), channel_id=1, source_target_pairs={{0,4},{4,0},{1,5},{5,1},{2,6},{6,2},{3,7},{7,3}} | collective-permute-start | bytes 9043976 | tf_op jit(solution)/shard_map/cond/branch_1_fun/ppermute | solution.py:332
  571.3 170.2 %collective-permute-start.30 = (bf16[736,2048]{1,0:T(8,128)(2,1)}, bf16[736,2048]{1,0:T(8,128)(2,1)}, u32[]{:S(2)}, u32[]{:S(2)}) collective-permute-start(bf16[736,2048]{1,0:T(8,128)(2,1)} %add_convert_fusion.14), channel_id=1, source_target_pairs={{0,2},{2,0},{1,3},{3,1},{4,6},{6,4},{5,7},{7,5}} | collective-permute-start | bytes 9043976 | tf_op jit(solution)/shard_map/cond/branch_1_fun/ppermute | solution.py:352
  694.2 99.2 %collective-permute-start.39 = (bf16[736,2048]{1,0:T(8,128)(2,1)}, bf16[736,2048]{1,0:T(8,128)(2,1)}, u32[]{:S(2)}, u32[]{:S(2)}) collective-permute-start(bf16[736,2048]{1,0:T(8,128)(2,1)} %get-tuple-element.246), channel_id=1, source_target_pairs={{0,4},{4,0},{1,5},{5,1},{2,6},{6,2},{3,7},{7,3}} | collective-permute-start | bytes 9043976 | tf_op jit(solution)/shard_map/cond/branch_1_fun/ppermute | solution.py:332
  702.2 27.6 %copy-start.50 = (bf16[736,2048]{1,0:T(8,128)(2,1)S(1)}, bf16[736,2048]{1,0:T(8,128)(2,1)}, u32[]{:S(2)}) copy-start(bf16[736,2048]{1,0:T(8,128)(2,1)} %get-tuple-element.239) | copy-start | bytes 9043972 | tf_op jit(solution)/shard_map/cond
  702.2 95.9 %collective-permute-start.34 = (bf16[736,2048]{1,0:T(8,128)(2,1)}, bf16[736,2048]{1,0:T(8,128)(2,1)}, u32[]{:S(2)}, u32[]{:S(2)}) collective-permute-start(bf16[736,2048]{1,0:T(8,128)(2,1)} %add_convert_fusion.12), channel_id=1, source_target_pairs={{0,2},{2,0},{1,3},{3,1},{4,6},{6,4},{5,7},{7,5}} | collective-permute-start | bytes 9043976 | tf_op jit(solution)/shard_map/cond/branch_1_fun/ppermute | solution.py:352
  728.8 129.2 %collective-permute-start.43 = (bf16[736,2048]{1,0:T(8,128)(2,1)}, bf16[736,2048]{1,0:T(8,128)(2,1)}, u32[]{:S(2)}, u32[]{:S(2)}) collective-permute-start(bf16[736,2048]{1,0:T(8,128)(2,1)} %get-tuple-element.252), channel_id=1, source_target_pairs={{0,4},{4,0},{1,5},{5,1},{2,6},{6,2},{3,7},{7,3}} | collective-permute-start | bytes 9043976 | tf_op jit(solution)/shard_map/cond/branch_1_fun/ppermute | solution.py:332
  734.7 187.9 %collective-permute-start.36 = (bf16[736,2048]{1,0:T(8,128)(2,1)}, bf16[736,2048]{1,0:T(8,128)(2,1)}, u32[]{:S(2)}, u32[]{:S(2)}) collective-permute-start(bf16[736,2048]{1,0:T(8,128)(2,1)} %get-tuple-element.234), channel_id=1, source_target_pairs={{0,4},{4,0},{1,5},{5,1},{2,6},{6,2},{3,7},{7,3}} | collective-permute-start | bytes 9043976 | tf_op jit(solution)/shard_map/cond/branch_1_fun/ppermute | solution.py:332
  741.4 245.7 %collective-permute-start.42 = (bf16[736,2048]{1,0:T(8,128)(2,1)}, bf16[736,2048]{1,0:T(8,128)(2,1)}, u32[]{:S(2)}, u32[]{:S(2)}) collective-permute-start(bf16[736,2048]{1,0:T(8,128)(2,1)} %get-tuple-element.250), channel_id=1, source_target_pairs={{0,4},{4,0},{1,5},{5,1},{2,6},{6,2},{3,7},{7,3}} | collective-permute-start | bytes 9043976 | tf_op jit(solution)/shard_map/cond/branch_1_fun/ppermute | solution.py:332
  741.4 51.9 %copy-start.47 = (bf16[736,2048]{1,0:T(8,128)(2,1)S(1)}, bf16[736,2048]{1,0:T(8,128)(2,1)}, u32[]{:S(2)}) copy-start(bf16[736,2048]{1,0:T(8,128)(2,1)} %get-tuple-element.247) | copy-start | bytes 9043972 | tf_op jit(solution)/shard_map/cond
  798.1 129.2 %collective-permute-start.40 = (bf16[736,2048]{1,0:T(8,128)(2,1)}, bf16[736,2048]{1,0:T(8,128)(2,1)}, u32[]{:S(2)}, u32[]{:S(2)}) collective-permute-start(bf16[736,2048]{1,0:T(8,128)(2,1)} %add_convert_fusion.10), channel_id=1, source_target_pairs={{0,2},{2,0},{1,3},{3,1},{4,6},{6,4},{5,7},{7,5}} | collective-permute-start | bytes 9043976 | tf_op jit(solution)/shard_map/cond/branch_1_fun/ppermute | solution.py:356
  858.0 64.6 %copy-start.48 = (bf16[736,2048]{1,0:T(8,128)(2,1)S(1)}, bf16[736,2048]{1,0:T(8,128)(2,1)}, u32[]{:S(2)}) copy-start(bf16[736,2048]{1,0:T(8,128)(2,1)} %get-tuple-element.243) | copy-start | bytes 9043972 | tf_op jit(solution)/shard_map/cond
  864.0 129.0 %collective-permute-start.44 = (bf16[736,2048]{1,0:T(8,128)(2,1)}, bf16[736,2048]{1,0:T(8,128)(2,1)}, u32[]{:S(2)}, u32[]{:S(2)}) collective-permute-start(bf16[736,2048]{1,0:T(8,128)(2,1)} %add_convert_fusion.8), channel_id=1, source_target_pairs={{0,2},{2,0},{1,3},{3,1},{4,6},{6,4},{5,7},{7,5}} | collective-permute-start | bytes 9043976 | tf_op jit(solution)/shard_map/cond/branch_1_fun/ppermute | solution.py:356
  864.0 168.1 %collective-permute-start.31 = (bf16[512,2048]{1,0:T(8,128)(2,1)S(1)}, bf16[512,2048]{1,0:T(8,128)(2,1)}, u32[]{:S(2)}, u32[]{:S(2)}) collective-permute-start(bf16[512,2048]{1,0:T(8,128)(2,1)S(1)} %copy-done.10), channel_id=1, source_target_pairs={{0,4},{4,0},{1,5},{5,1},{2,6},{6,2},{3,7},{7,3}} | collective-permute-start | bytes 6291464 | tf_op jit(solution)/shard_map/cond/branch_1_fun/ppermute | solution.py:340
  927.3 149.7 %collective-permute-start.35 = (bf16[512,2048]{1,0:T(8,128)(2,1)}, bf16[512,2048]{1,0:T(8,128)(2,1)}, u32[]{:S(2)}, u32[]{:S(2)}) collective-permute-start(bf16[512,2048]{1,0:T(8,128)(2,1)} %branch_1_fun.14), channel_id=1, source_target_pairs={{0,4},{4,0},{1,5},{5,1},{2,6},{6,2},{3,7},{7,3}} | collective-permute-start | bytes 6291464 | tf_op jit(solution)/shard_map/cond/branch_1_fun/ppermute | solution.py:340
  939.5 182.5 %collective-permute-start.41 = (bf16[512,2048]{1,0:T(8,128)(2,1)}, bf16[512,2048]{1,0:T(8,128)(2,1)}, u32[]{:S(2)}, u32[]{:S(2)}) collective-permute-start(bf16[512,2048]{1,0:T(8,128)(2,1)} %branch_1_fun.16), channel_id=1, source_target_pairs={{0,4},{4,0},{1,5},{5,1},{2,6},{6,2},{3,7},{7,3}} | collective-permute-start | bytes 6291464 | tf_op jit(solution)/shard_map/cond/branch_1_fun/ppermute | solution.py:340
  1004.9 145.6 %collective-permute-start.45 = (bf16[512,2048]{1,0:T(8,128)(2,1)}, bf16[512,2048]{1,0:T(8,128)(2,1)}, u32[]{:S(2)}, u32[]{:S(2)}) collective-permute-start(bf16[512,2048]{1,0:T(8,128)(2,1)} %branch_1_fun.17), channel_id=1, source_target_pairs={{0,4},{4,0},{1,5},{5,1},{2,6},{6,2},{3,7},{7,3}} | collective-permute-start | bytes 6291464 | tf_op jit(solution)/shard_map/cond/branch_1_fun/ppermute | solution.py:340
  1035.3 44.9 %copy-start.14 = (bf16[512,2048]{1,0:T(8,128)(2,1)S(1)}, bf16[512,2048]{1,0:T(8,128)(2,1)}, u32[]{:S(2)}) copy-start(bf16[512,2048]{1,0:T(8,128)(2,1)} %branch_1_fun.16) | copy-start | bytes 6291460 | tf_op jit(solution)/shard_map/cond
  1080.2 44.9 %copy-start.18 = (bf16[512,2048]{1,0:T(8,128)(2,1)S(1)}, bf16[512,2048]{1,0:T(8,128)(2,1)}, u32[]{:S(2)}) copy-start(bf16[512,2048]{1,0:T(8,128)(2,1)} %branch_1_fun.17) | copy-start | bytes 6291460 | tf_op jit(solution)/shard_map/cond
  (11 other events, 93.3 us)
